TPU v7x, 32 devices: a whole 2x2x4 slice. The times are simulated.
32 devices in a mesh: section: 4 (over y, x), seq: 2 (over core), tensor: 4 (over z).
Axes of the slice: x: 2, y: 2, z: 4, core: 2. Of those that a mesh axis runs over, the one named last changes fastest.
Arguments:
- states_in: bfloat16 [1, 256, 4608], P(None, 'seq', 'tensor'), may hold values from -100 to 100
- span_order: int32 [4], replicated, may hold values from 0 to 3, each once
- pre_gain: bfloat16 [4, 4608], P('section'), may hold values from 0.25 to 1.75
- w_query: bfloat16 [4, 4608, 4096], P('section', None, 'tensor'), may hold values from -0.09375 to 0.09375
- w_key: bfloat16 [4, 4608, 2048], P('section', None, 'tensor'), may hold values from -0.09375 to 0.09375
- w_value: bfloat16 [4, 4608, 2048], P('section', None, 'tensor'), may hold values from -0.09375 to 0.09375
- w_out: bfloat16 [4, 4096, 4608], P('section', 'tensor'), may hold values from -0.125 to 0.125
- post_gain: bfloat16 [4, 4608], P('section'), may hold values from 0.25 to 1.75
Outputs:
- states: bfloat16 [4, 1, 256, 4608], P('section', None, 'seq', 'tensor')
Inputs may be any that keep to these rules, and one draw needn't show every extreme that they name: Each span number appears once; row block j of 64 rows holds the tokens from position span_order[j] * 64 on.
All inputs are finite; a program needn't handle non-finite values.
Results may differ from a plain program's by a relative error of at most 0.024.
Values may be sent and summed in bfloat16 or wider, within the bound.
A program may use at most 128 MiB of HBM per device.

v0:
```python
import jax
import jax.numpy as jnp
from jax import lax
from jax.sharding import PartitionSpec as P

HEAD_DIM = 128


softcap_limit = 50.0
query_scale = 144.0 ** (-0.5)
epsilon = 1e-06
rotary_base = 10000.0


def from_behind(value, axis, steps):
    count = lax.axis_size(axis)
    first, last = (max(0, -steps), min(count, count - steps))
    return lax.ppermute(value, axis, [(source, source + steps) for source in range(first, last)])


def rotate(vectors, places):
    half_dim = vectors.shape[-1] // 2
    inverse = rotary_base ** (-(jnp.arange(half_dim, dtype=jnp.float32) * 2.0 / vectors.shape[-1]))
    angles = places.astype(jnp.float32)[:, None] * inverse[None, :]
    cos_part = jnp.cos(angles)[:, None, :]
    sin_part = jnp.sin(angles)[:, None, :]
    lower_half = vectors[..., :half_dim]
    upper_half = vectors[..., half_dim:]
    return jnp.concatenate(
        [
            lower_half * cos_part - upper_half * sin_part,
            upper_half * cos_part + lower_half * sin_part,
        ],
        axis=-1,
    )


def span_positions(first_row, row_total, order_table, span_rows):
    row_ids = first_row + jnp.arange(row_total, dtype=jnp.int32)
    blocks = row_ids // span_rows
    matches = blocks[:, None] == jnp.arange(order_table.shape[0], dtype=jnp.int32)[None, :]
    starts = jnp.sum(jnp.where(matches, order_table[None, :], 0), axis=1)
    return starts * span_rows + row_ids % span_rows


def body(states_in, span_order, pre_gain, w_query, w_key, w_value, w_out, post_gain):
    micro_count, row_count, width_part = states_in.shape
    model_width = pre_gain.shape[1]
    head_size = HEAD_DIM
    kv_local = w_key.shape[2] // head_size
    q_local = w_query.shape[2] // head_size
    group_size = q_local // kv_local
    span_rows = row_count // 2
    section_count = lax.axis_size("section")
    section_rank = lax.axis_index("section")
    seq_rank = lax.axis_index("seq")
    tensor_rank = lax.axis_index("tensor")
    tick_total = section_count + micro_count - 1
    query_places = span_positions(seq_rank * row_count, row_count, span_order, span_rows)
    gain_in = pre_gain[0].astype(jnp.float32)
    gain_out = post_gain[0].astype(jnp.float32)

    def layer(full_rows):
        stream = full_rows.astype(jnp.float32)
        normed = (
            stream * lax.rsqrt(jnp.mean(stream * stream, axis=1, keepdims=True) + epsilon) * gain_in
        ).astype(jnp.bfloat16)
        queries = jnp.dot(normed, w_query[0], preferred_element_type=jnp.float32).reshape(
            row_count, q_local, head_size
        )
        queries = (
            (rotate(queries, query_places) * query_scale)
            .astype(jnp.bfloat16)
            .reshape(row_count, kv_local, group_size, head_size)
        )
        key_rows = jnp.dot(normed, w_key[0], preferred_element_type=jnp.float32).reshape(
            row_count, kv_local, head_size
        )
        key_rows = (
            rotate(key_rows, query_places)
            .astype(jnp.bfloat16)
            .reshape(row_count, kv_local * head_size)
        )
        values = jnp.dot(normed, w_value[0], preferred_element_type=jnp.float32).astype(
            jnp.bfloat16
        )
        key_piece = lax.all_gather(key_rows, "seq", axis=0, tiled=True)
        value_piece = lax.all_gather(values, "seq", axis=0, tiled=True)
        key_count = key_piece.shape[0]
        key_places = span_positions(jnp.int32(0), key_count, span_order, span_rows)
        scores = jnp.einsum(
            "tkgd,pkd->kgtp",
            queries,
            key_piece.reshape(key_count, kv_local, head_size),
            preferred_element_type=jnp.float32,
        )
        capped = softcap_limit * jnp.tanh(scores / softcap_limit)
        allowed = key_places[None, :] <= query_places[:, None]
        weight = jnp.where(allowed[None, None], jnp.exp(capped), jnp.float32(0.0))
        totals = jnp.sum(weight, axis=3)
        numerator = jnp.einsum(
            "kgtp,pkd->tkgd",
            weight.astype(jnp.bfloat16),
            value_piece.reshape(key_count, kv_local, head_size),
            preferred_element_type=jnp.float32,
        )
        numerator, totals = (numerator, totals)
        attended = (
            (numerator / jnp.transpose(totals, (2, 0, 1))[..., None])
            .astype(jnp.bfloat16)
            .reshape(row_count, q_local * head_size)
        )
        partial_value = jnp.dot(attended, w_out[0], preferred_element_type=jnp.float32)
        projected = lax.psum(partial_value.astype(jnp.bfloat16), "tensor").astype(jnp.float32)
        scaling = lax.rsqrt(jnp.mean(projected * projected, axis=1, keepdims=True) + epsilon)
        new_full = (stream + projected * scaling * gain_out).astype(jnp.bfloat16)
        new_part = lax.dynamic_slice_in_dim(new_full, tensor_rank * width_part, width_part, 1)
        return (new_part, new_full)

    def take_micro(tick_index):
        return lax.dynamic_index_in_dim(
            states_in, jnp.minimum(tick_index, micro_count - 1), 0, keepdims=False
        )

    def tick(carried, tick_index):
        outgoing, record = carried
        arrived = from_behind(outgoing, "section", 1)
        entering = lax.all_gather(take_micro(tick_index), "tensor", axis=1, tiled=True)
        full_rows = jnp.where(section_rank == 0, entering, arrived)
        new_part, new_full = layer(full_rows)
        slot_index = tick_index - section_rank
        is_valid = jnp.logical_and(slot_index >= 0, slot_index < micro_count)
        placed = lax.dynamic_update_index_in_dim(
            record, new_part, jnp.clip(slot_index, 0, micro_count - 1), 0
        )
        record = jnp.where(is_valid, placed, record)
        outgoing = new_full
        return ((outgoing, record), None)

    first_out = jnp.zeros((row_count, model_width), jnp.bfloat16)
    first_record = jnp.zeros((micro_count, row_count, width_part), jnp.bfloat16)
    (last_out, record), unused = lax.scan(
        tick, (first_out, first_record), jnp.arange(tick_total, dtype=jnp.int32)
    )
    return record[None]


def solution(mesh):
    in_specs = (
        P(None, "seq", "tensor"),
        P(),
        P("section", None),
        P("section", None, "tensor"),
        P("section", None, "tensor"),
        P("section", None, "tensor"),
        P("section", "tensor", None),
        P("section", None),
    )
    out_specs = P("section", None, "seq", "tensor")
    return jax.shard_map(body, mesh=mesh, in_specs=in_specs, out_specs=out_specs, check_vma=False)
```

profile of v0, /device:TPU:30, one launch (start us, length us, event | category | flops | bytes accessed | tf_op | source)
XLA Modules:
  0.0 495.1 jit_solution(17398841147142758691)
XLA Ops:
  8.8 12.7 %copy.28 = bf16[1,4608,1024]{1,2,0:T(8,128)(2,1)} copy(bf16[1,4608,1024]{2,1,0:T(8,128)(2,1)} %param.13) | data formatting | bytes 18874368
  21.5 6.8 %copy.27 = bf16[1,4608,512]{1,2,0:T(8,128)(2,1)} copy(bf16[1,4608,512]{2,1,0:T(8,128)(2,1)} %param.14) | data formatting | bytes 9437184
  28.3 459.3 %while.15 = (s32[]{:T(128)}, bf16[128,4608]{1,0:T(8,128)(2,1)S(1)}, bf16[1,128,1152]{2,1,0:T(8,128)(2,1)S(1)}, pred[]{:T(512)}, bf16[1,128,1152]{2,1,0:T(8,128)(...) while((s32[]{:T(128)}, bf16[128,4608]{1,0:T(8,128)(2,1)S(1)}, ...), condition=%wide.region_7.8_spmd.clone, body=%wide.region_1.7_spmd.clone.sunk | while | flops 3777902848 | bytes 106681320 | solution.py:142
  30.9 27.9 %collective-permute-done = bf16[128,4608]{1,0:T(8,128)(2,1)S(1)} collective-permute-done((bf16[128,4608]{1,0:T(8,128)(2,1)S(1)}, bf16[128,4608]{1,0:T(8,128)(2,1)S(1)}, u32[]{:S(2)}, u32[]{:S(2)}) %collective-permute-start) | collective-permute-done | bytes 1179680 | tf_op jit(solution)/shard_map/while/body/eval_jaxpr/ppermute | solution.py:18
  62.1 4.2 fusion.84
  71.6 3.2 fusion.83
  77.8 6.2 %fusion.89 = bf16[128,4608]{1,0:T(8,128)(2,1)} fusion(bf16[128,1024]{0,1:T(8,128)(2,1)S(1)} %bitcast.117, bf16[1,1024,4608]{2,1,0:T(8,128)(2,1)} %get-tuple-element.538), kind=kOutput, calls=%fused_computation.2.clone.1 | convolution fusion | flops 1208549376 | bytes 10878976 | tf_op jit(solution)/shard_map/while/body/eval_jaxpr/dot_general | solution.py:113
  85.3 54.3 %all-reduce.2.cloned.1.call-done = bf16[128,4608]{1,0:T(8,128)(2,1)} async-done(((bf16[128,4608]{1,0:T(8,128)(2,1)}), bf16[128,4608]{1,0:T(8,128)(2,1)}) %all-reduce.2.cloned.1.call-update) | async-done | bytes 1179664 | tf_op jit(solution)/shard_map/while/body/eval_jaxpr/psum | solution.py:114
  145.8 28.0 %collective-permute-done = bf16[128,4608]{1,0:T(8,128)(2,1)S(1)} collective-permute-done((bf16[128,4608]{1,0:T(8,128)(2,1)S(1)}, bf16[128,4608]{1,0:T(8,128)(2,1)S(1)}, u32[]{:S(2)}, u32[]{:S(2)}) %collective-permute-start) | collective-permute-done | bytes 1179680 | tf_op jit(solution)/shard_map/while/body/eval_jaxpr/ppermute | solution.py:18
  177.0 4.2 fusion.84
  186.5 3.2 fusion.83
  192.8 6.2 %fusion.89 = bf16[128,4608]{1,0:T(8,128)(2,1)} fusion(bf16[128,1024]{0,1:T(8,128)(2,1)S(1)} %bitcast.117, bf16[1,1024,4608]{2,1,0:T(8,128)(2,1)} %get-tuple-element.538), kind=kOutput, calls=%fused_computation.2.clone.1 | convolution fusion | flops 1208549376 | bytes 10878976 | tf_op jit(solution)/shard_map/while/body/eval_jaxpr/dot_general | solution.py:113
  200.3 54.3 %all-reduce.2.cloned.1.call-done = bf16[128,4608]{1,0:T(8,128)(2,1)} async-done(((bf16[128,4608]{1,0:T(8,128)(2,1)}), bf16[128,4608]{1,0:T(8,128)(2,1)}) %all-reduce.2.cloned.1.call-update) | async-done | bytes 1179664 | tf_op jit(solution)/shard_map/while/body/eval_jaxpr/psum | solution.py:114
  260.5 28.0 %collective-permute-done = bf16[128,4608]{1,0:T(8,128)(2,1)S(1)} collective-permute-done((bf16[128,4608]{1,0:T(8,128)(2,1)S(1)}, bf16[128,4608]{1,0:T(8,128)(2,1)S(1)}, u32[]{:S(2)}, u32[]{:S(2)}) %collective-permute-start) | collective-permute-done | bytes 1179680 | tf_op jit(solution)/shard_map/while/body/eval_jaxpr/ppermute | solution.py:18
  291.6 4.2 fusion.84
  298.0 2.7 fusion.85
  301.1 3.2 fusion.83
  307.3 6.2 %fusion.89 = bf16[128,4608]{1,0:T(8,128)(2,1)} fusion(bf16[128,1024]{0,1:T(8,128)(2,1)S(1)} %bitcast.117, bf16[1,1024,4608]{2,1,0:T(8,128)(2,1)} %get-tuple-element.538), kind=kOutput, calls=%fused_computation.2.clone.1 | convolution fusion | flops 1208549376 | bytes 10878976 | tf_op jit(solution)/shard_map/while/body/eval_jaxpr/dot_general | solution.py:113
  314.8 54.3 %all-reduce.2.cloned.1.call-done = bf16[128,4608]{1,0:T(8,128)(2,1)} async-done(((bf16[128,4608]{1,0:T(8,128)(2,1)}), bf16[128,4608]{1,0:T(8,128)(2,1)}) %all-reduce.2.cloned.1.call-update) | async-done | bytes 1179664 | tf_op jit(solution)/shard_map/while/body/eval_jaxpr/psum | solution.py:114
  375.3 28.0 %collective-permute-done = bf16[128,4608]{1,0:T(8,128)(2,1)S(1)} collective-permute-done((bf16[128,4608]{1,0:T(8,128)(2,1)S(1)}, bf16[128,4608]{1,0:T(8,128)(2,1)S(1)}, u32[]{:S(2)}, u32[]{:S(2)}) %collective-permute-start) | collective-permute-done | bytes 1179680 | tf_op jit(solution)/shard_map/while/body/eval_jaxpr/ppermute | solution.py:18
  406.5 4.2 fusion.84
  416.0 3.2 fusion.83
  422.3 6.2 %fusion.89 = bf16[128,4608]{1,0:T(8,128)(2,1)} fusion(bf16[128,1024]{0,1:T(8,128)(2,1)S(1)} %bitcast.117, bf16[1,1024,4608]{2,1,0:T(8,128)(2,1)} %get-tuple-element.538), kind=kOutput, calls=%fused_computation.2.clone.1 | convolution fusion | flops 1208549376 | bytes 10878976 | tf_op jit(solution)/shard_map/while/body/eval_jaxpr/dot_general | solution.py:113
  429.8 54.3 %all-reduce.2.cloned.1.call-done = bf16[128,4608]{1,0:T(8,128)(2,1)} async-done(((bf16[128,4608]{1,0:T(8,128)(2,1)}), bf16[128,4608]{1,0:T(8,128)(2,1)}) %all-reduce.2.cloned.1.call-update) | async-done | bytes 1179664 | tf_op jit(solution)/shard_map/while/body/eval_jaxpr/psum | solution.py:114
  (167 shorter events, 73.0 us)
Async XLA Ops:
  28.3 43.4 %copy-start.3 = (f32[4608]{0:T(1024)}, f32[4608]{0:T(1024)S(1)}, u32[]{:S(2)}) copy-start(f32[4608]{0:T(1024)S(1)} %get-tuple-element.531) | copy-start | bytes 55300 | tf_op jit(solution)/shard_map/while
  28.3 31.9 %all-gather.6.cloned.1.call-start = ((), (), s32[]{:S(2)}) async-start(), calls=%async_computation | async-start | bytes 1474560 | tf_op jit(solution)/shard_map/while/body/eval_jaxpr/all_gather | solution.py:128
  29.0 110.6 %all-reduce.2.cloned.1.call-start = ((), (), s32[]{:S(2)}) async-start(), calls=%async_computation.1 | async-start | bytes 2359296 | tf_op jit(solution)/shard_map/while/body/eval_jaxpr/psum | solution.py:114
  29.2 29.6 %collective-permute-start = (bf16[128,4608]{1,0:T(8,128)(2,1)S(1)}, bf16[128,4608]{1,0:T(8,128)(2,1)S(1)}, u32[]{:S(2)}, u32[]{:S(2)}) collective-permute-start(bf16[128,4608]{1,0:T(8,128)(2,1)S(1)} %broadcast_select_fusion.2), channel_id=1, source_target_pairs={{0,8},{8,16},{16,24},{1,9},{9,17},{17,25},{2,10},{10,18},{18,26},{... | collective-permute-start | bytes 3538952 | tf_op jit(solution)/shard_map/while/body/eval_jaxpr/ppermute | solution.py:18
  60.2 8.3 %copy-start = (bf16[1,4608,1024]{1,2,0:T(8,128)(2,1)S(1)}, bf16[1,4608,1024]{1,2,0:T(8,128)(2,1)}, u32[]{:S(2)}) copy-start(bf16[1,4608,1024]{1,2,0:T(8,128)(2,1)} %get-tuple-element.537) | copy-start | bytes 28311556 | tf_op jit(solution)/shard_map/while
  84.0 57.2 %copy-start.2 = (f32[4608]{0:T(1024)S(1)}, f32[4608]{0:T(1024)}, u32[]{:S(2)}) copy-start(f32[4608]{0:T(1024)} %get-tuple-element.539) | copy-start | bytes 55300 | tf_op jit(solution)/shard_map/while
  143.2 43.4 %copy-start.3 = (f32[4608]{0:T(1024)}, f32[4608]{0:T(1024)S(1)}, u32[]{:S(2)}) copy-start(f32[4608]{0:T(1024)S(1)} %get-tuple-element.531) | copy-start | bytes 55300 | tf_op jit(solution)/shard_map/while
  143.2 31.9 %all-gather.6.cloned.1.call-start = ((), (), s32[]{:S(2)}) async-start(), calls=%async_computation | async-start | bytes 1474560 | tf_op jit(solution)/shard_map/while/body/eval_jaxpr/all_gather | solution.py:128
  143.9 110.6 %all-reduce.2.cloned.1.call-start = ((), (), s32[]{:S(2)}) async-start(), calls=%async_computation.1 | async-start | bytes 2359296 | tf_op jit(solution)/shard_map/while/body/eval_jaxpr/psum | solution.py:114
  144.0 29.7 %collective-permute-start = (bf16[128,4608]{1,0:T(8,128)(2,1)S(1)}, bf16[128,4608]{1,0:T(8,128)(2,1)S(1)}, u32[]{:S(2)}, u32[]{:S(2)}) collective-permute-start(bf16[128,4608]{1,0:T(8,128)(2,1)S(1)} %broadcast_select_fusion.2), channel_id=1, source_target_pairs={{0,8},{8,16},{16,24},{1,9},{9,17},{17,25},{2,10},{10,18},{18,26},{... | collective-permute-start | bytes 3538952 | tf_op jit(solution)/shard_map/while/body/eval_jaxpr/ppermute | solution.py:18
  175.1 8.3 %copy-start = (bf16[1,4608,1024]{1,2,0:T(8,128)(2,1)S(1)}, bf16[1,4608,1024]{1,2,0:T(8,128)(2,1)}, u32[]{:S(2)}) copy-start(bf16[1,4608,1024]{1,2,0:T(8,128)(2,1)} %get-tuple-element.537) | copy-start | bytes 28311556 | tf_op jit(solution)/shard_map/while
  198.9 57.2 %copy-start.2 = (f32[4608]{0:T(1024)S(1)}, f32[4608]{0:T(1024)}, u32[]{:S(2)}) copy-start(f32[4608]{0:T(1024)} %get-tuple-element.539) | copy-start | bytes 55300 | tf_op jit(solution)/shard_map/while
  258.1 43.1 %copy-start.3 = (f32[4608]{0:T(1024)}, f32[4608]{0:T(1024)S(1)}, u32[]{:S(2)}) copy-start(f32[4608]{0:T(1024)S(1)} %get-tuple-element.531) | copy-start | bytes 55300 | tf_op jit(solution)/shard_map/while
  258.1 31.6 %all-gather.6.cloned.1.call-start = ((), (), s32[]{:S(2)}) async-start(), calls=%async_computation | async-start | bytes 1474560 | tf_op jit(solution)/shard_map/while/body/eval_jaxpr/all_gather | solution.py:128
  258.6 110.5 %all-reduce.2.cloned.1.call-start = ((), (), s32[]{:S(2)}) async-start(), calls=%async_computation.1 | async-start | bytes 2359296 | tf_op jit(solution)/shard_map/while/body/eval_jaxpr/psum | solution.py:114
  258.8 29.7 %collective-permute-start = (bf16[128,4608]{1,0:T(8,128)(2,1)S(1)}, bf16[128,4608]{1,0:T(8,128)(2,1)S(1)}, u32[]{:S(2)}, u32[]{:S(2)}) collective-permute-start(bf16[128,4608]{1,0:T(8,128)(2,1)S(1)} %broadcast_select_fusion.2), channel_id=1, source_target_pairs={{0,8},{8,16},{16,24},{1,9},{9,17},{17,25},{2,10},{10,18},{18,26},{... | collective-permute-start | bytes 3538952 | tf_op jit(solution)/shard_map/while/body/eval_jaxpr/ppermute | solution.py:18
  289.7 8.3 %copy-start = (bf16[1,4608,1024]{1,2,0:T(8,128)(2,1)S(1)}, bf16[1,4608,1024]{1,2,0:T(8,128)(2,1)}, u32[]{:S(2)}) copy-start(bf16[1,4608,1024]{1,2,0:T(8,128)(2,1)} %get-tuple-element.537) | copy-start | bytes 28311556 | tf_op jit(solution)/shard_map/while
  313.5 57.2 %copy-start.2 = (f32[4608]{0:T(1024)S(1)}, f32[4608]{0:T(1024)}, u32[]{:S(2)}) copy-start(f32[4608]{0:T(1024)} %get-tuple-element.539) | copy-start | bytes 55300 | tf_op jit(solution)/shard_map/while
  372.6 43.4 %copy-start.3 = (f32[4608]{0:T(1024)}, f32[4608]{0:T(1024)S(1)}, u32[]{:S(2)}) copy-start(f32[4608]{0:T(1024)S(1)} %get-tuple-element.531) | copy-start | bytes 55300 | tf_op jit(solution)/shard_map/while
  372.7 31.9 %all-gather.6.cloned.1.call-start = ((), (), s32[]{:S(2)}) async-start(), calls=%async_computation | async-start | bytes 1474560 | tf_op jit(solution)/shard_map/while/body/eval_jaxpr/all_gather | solution.py:128
  373.4 110.6 %all-reduce.2.cloned.1.call-start = ((), (), s32[]{:S(2)}) async-start(), calls=%async_computation.1 | async-start | bytes 2359296 | tf_op jit(solution)/shard_map/while/body/eval_jaxpr/psum | solution.py:114
  373.5 29.7 %collective-permute-start = (bf16[128,4608]{1,0:T(8,128)(2,1)S(1)}, bf16[128,4608]{1,0:T(8,128)(2,1)S(1)}, u32[]{:S(2)}, u32[]{:S(2)}) collective-permute-start(bf16[128,4608]{1,0:T(8,128)(2,1)S(1)} %broadcast_select_fusion.2), channel_id=1, source_target_pairs={{0,8},{8,16},{16,24},{1,9},{9,17},{17,25},{2,10},{10,18},{18,26},{... | collective-permute-start | bytes 3538952 | tf_op jit(solution)/shard_map/while/body/eval_jaxpr/ppermute | solution.py:18
  404.6 8.3 %copy-start = (bf16[1,4608,1024]{1,2,0:T(8,128)(2,1)S(1)}, bf16[1,4608,1024]{1,2,0:T(8,128)(2,1)}, u32[]{:S(2)}) copy-start(bf16[1,4608,1024]{1,2,0:T(8,128)(2,1)} %get-tuple-element.537) | copy-start | bytes 28311556 | tf_op jit(solution)/shard_map/while
  428.4 57.2 %copy-start.2 = (f32[4608]{0:T(1024)S(1)}, f32[4608]{0:T(1024)}, u32[]{:S(2)}) copy-start(f32[4608]{0:T(1024)} %get-tuple-element.539) | copy-start | bytes 55300 | tf_op jit(solution)/shard_map/while
  (6 other events, 15.2 us)
Sparse Core Ops, SparseCore 0:
  30.7 29.4 all-gather.5
  84.2 55.4 all-reduce.1
  145.6 29.4 all-gather.5
  199.1 55.3 all-reduce.1
  260.2 29.4 all-gather.5
  313.7 55.3 all-reduce.1
  375.1 29.4 all-gather.5
  428.6 55.3 all-reduce.1
where the time goes:
time: 500 us; the launch traced here: 495 us
  waiting for transfers between devices  337 us (67%)
  matrix products  68.5 us (14%)
  other arithmetic  26.3 us (5%)
  local copies, waits for them, and re-layouts  25 us (5%)
  blocking collectives  16.1 us (3%)
  between operations  13.4 us (3%)
  starting transfers between devices  5.48 us (1%)
    psum x4, waiting for transfers between devices, layer(): lax.psum(partial_value.astype(jnp.bfloat16), 'tensor').astype(jnp.float32)  217 us
    ppermute x4, waiting for transfers between devices, from_behind(): lax.ppermute(value, axis, [(source, source + steps) for source in range(f...  112 us
    dot_general x4, matrix products, layer(): jnp.dot(attended, w_out[0], preferred_element_type=jnp.float32)  24.7 us
    unnamed x6, local copies, waits for them, and re-layouts  20.2 us
    dot_general x4, matrix products, layer(): jnp.dot(normed, w_key[0], preferred_element_type=jnp.float32)  16.9 us
    dot_general x4, matrix products, layer(): jnp.dot(normed, w_value[0], preferred_element_type=jnp.float32)  12.6 us
    dot_general x4, matrix products, layer(): jnp.dot(normed, w_query[0], preferred_element_type=jnp.float32)  10.6 us
  transfers between devices with their start and end apart: 12, of which 12 were waited for; matrix products, arithmetic and copies ran while one was open for 1% of the time, Pallas kernels for 0%

commit v1 on v0

v1 whole, which is shorter than its diff:
```python
import functools
import math

import jax
import jax.numpy as jnp
from jax import lax
from jax.experimental import pallas as pl
from jax.experimental.pallas import tpu as pltpu
from jax.sharding import PartitionSpec as P

HEAD_DIM = 128

softcap_limit = 50.0
query_scale = 144.0 ** (-0.5)
epsilon = 1e-06
rotary_base = 10000.0

MESH = pl.DeviceIdType.MESH
f32 = jnp.float32
bf16 = jnp.bfloat16


def kernel(
    sections, seqs, tensors,
    states, order, gain_in, wq_hbm, wk_hbm, wv_hbm, wo_hbm, gain_out, out,
    wq, wk, wv, wo, x, acc_q, acc_kv, kv, qh, att, part, from_left, from_right, total, fresh, landed,
    w_sem, x0_recv, x0_right, x0_left, x_recv, x_right, x_left, kv_send, kv_recv,
    l_recv, r_recv, l_send, r_send, next_send, out_send, out_recv,
):
    s = lax.axis_index("section")
    q = lax.axis_index("seq")
    z = lax.axis_index("tensor")
    _, rows, width = states.shape
    chunks = x.shape[0]
    model = chunks * width
    part_rows = rows // tensors
    q_width = wq.shape[1]
    kv_width = wk.shape[1]
    q_heads = q_width // HEAD_DIM
    kv_heads = kv_width // HEAD_DIM
    group = q_heads // kv_heads
    span_count = order.shape[0]
    span = rows * seqs // span_count

    def remote(src, dst, send, recv, device):
        return pltpu.make_async_remote_copy(
            src_ref=src, dst_ref=dst, send_sem=send, recv_sem=recv, device_id=device, device_id_type=MESH
        )

    right = {"tensor": lax.rem(z + 1, tensors)}
    left = {"tensor": lax.rem(z + tensors - 1, tensors)}
    after = {"section": lax.rem(s + 1, sections)}

    loads = [
        pltpu.make_async_copy(src.at[0], dst, w_sem.at[i])
        for i, (src, dst) in enumerate(((wk_hbm, wk), (wv_hbm, wv), (wq_hbm, wq), (wo_hbm, wo)))
    ]
    for load in loads:
        load.start()

    barrier = pltpu.get_barrier_semaphore()
    for step in range(1, tensors):
        pl.semaphore_signal(barrier, inc=1, device_id={"tensor": lax.rem(z + step, tensors)}, device_id_type=MESH)
    for step in range(1, seqs):
        pl.semaphore_signal(barrier, inc=1, device_id={"seq": lax.rem(q + step, seqs)}, device_id_type=MESH)
    pl.semaphore_signal(barrier, inc=1, device_id=after, device_id_type=MESH)
    pl.semaphore_signal(barrier, inc=1, device_id={"section": lax.rem(s + sections - 1, sections)}, device_id_type=MESH)
    pl.semaphore_wait(barrier, tensors - 1 + seqs - 1 + 2)

    def block(o):
        return pl.ds(pl.multiple_of(o * part_rows, part_rows), part_rows)

    def first_right(o, src):
        return remote(src, x.at[o], x0_right.at[o], x0_recv.at[o], right)

    def first_left(o, src):
        return remote(src, x.at[o], x0_left.at[o], x0_recv.at[o], left)

    @pl.when(s == 0)
    def _():
        @pl.when(z < tensors - 1)
        def _():
            first_right(z, states.at[0]).start()

        @pl.when(z > 0)
        def _():
            first_left(z, states.at[0]).start()

        x[z] = states[0]

    row = lax.broadcasted_iota(jnp.int32, (rows, HEAD_DIM), 0) + q * rows
    starts = jnp.zeros((rows, HEAD_DIM), jnp.int32)
    key_col = lax.broadcasted_iota(jnp.int32, (1, rows * seqs), 1)
    key_starts = jnp.zeros((1, rows * seqs), jnp.int32)
    for j in range(span_count):
        begin = order[j] * span
        starts = jnp.where(row // span == j, begin, starts)
        key_starts = jnp.where(key_col // span == j, begin, key_starts)
    places = starts + row % span
    key_places = key_starts + key_col % span
    half = HEAD_DIM // 2
    lane = lax.broadcasted_iota(jnp.int32, (rows, HEAD_DIM), 1)
    inverse = jnp.exp((lane % half).astype(f32) * (-2.0 / HEAD_DIM * math.log(rotary_base)))
    angles = places.astype(f32) * inverse
    cos = jnp.cos(angles)
    sin = jnp.sin(angles) * jnp.where(lane < half, -1.0, 1.0)

    def rope(u):
        return u * cos + pltpu.roll(u, half, 1) * sin

    @pl.when(s == 0)
    def _():
        for d in range(1, tensors):
            @pl.when(z >= d)
            def _():
                first_right(z - d, x.at[z - d]).wait_recv()

                @pl.when(z < tensors - 1)
                def _():
                    first_right(z - d, x.at[z - d]).start()

            @pl.when(z + d < tensors)
            def _():
                first_left(z + d, x.at[z + d]).wait_recv()

                @pl.when(z > 0)
                def _():
                    first_left(z + d, x.at[z + d]).start()

    def piece(c, o, send, device):
        ref = x.at[c, block(o)]
        return remote(ref, ref, send.at[c, o], x_recv.at[c, o], device)

    acc_q[...] = jnp.zeros_like(acc_q)
    acc_kv[...] = jnp.zeros_like(acc_kv)
    for load in loads[:3]:
        load.wait()

    def finish_kv(scale):
        for k in range(kv_heads):
            cols = pl.ds(k * HEAD_DIM, HEAD_DIM)
            kv[q, :, cols] = rope(acc_kv[:, cols] * scale).astype(bf16)
        kv[q, :, kv_width:] = (acc_kv[:, kv_width:] * scale).astype(bf16)

    def take_chunk(c, squares):
        @pl.when(s > 0)
        def _():
            for d in range(tensors):
                if d == 0:
                    piece(c, z, x_right, right).wait_recv()

                    @pl.when(z < tensors - 1)
                    def _():
                        piece(c, z, x_right, right).start()

                    @pl.when(z > 0)
                    def _():
                        piece(c, z, x_left, left).start()
                else:
                    @pl.when(z >= d)
                    def _():
                        piece(c, z - d, x_right, right).wait_recv()

                        @pl.when(z < tensors - 1)
                        def _():
                            piece(c, z - d, x_right, right).start()

                    @pl.when(z + d < tensors)
                    def _():
                        piece(c, z + d, x_left, left).wait_recv()

                        @pl.when(z > 0)
                        def _():
                            piece(c, z + d, x_left, left).start()

        stream = x[c].astype(f32)
        squares = squares + jnp.sum(stream * stream, axis=1, keepdims=True)
        scaled = (stream * gain_in[c].astype(f32)).astype(bf16)
        depth = pl.ds(pl.multiple_of(c * width, width), width)
        acc_kv[:, :kv_width] += jnp.dot(scaled, wk[depth, :], preferred_element_type=f32)
        acc_kv[:, kv_width:] += jnp.dot(scaled, wv[depth, :], preferred_element_type=f32)
        acc_q[...] += jnp.dot(scaled, wq[depth, :], preferred_element_type=f32)
        return squares

    squares = lax.fori_loop(0, chunks, take_chunk, jnp.zeros((rows, 1), f32))
    scale = lax.rsqrt(squares / model + epsilon)
    finish_kv(scale)

    def kv_copy(j, device):
        return remote(kv.at[j], kv.at[j], kv_send.at[device], kv_recv.at[j], {"seq": device})

    for step in range(1, seqs):
        kv_copy(q, lax.rem(q + step, seqs)).start()
    for h in range(q_heads):
        cols = pl.ds(h * HEAD_DIM, HEAD_DIM)
        qh[:, cols] = (rope(acc_q[:, cols] * scale) * query_scale).astype(bf16)
    for step in range(1, seqs):
        other = lax.rem(q + step, seqs)
        kv_copy(other, other).wait_recv()

    dims = (((1,), (1,)), ((), ()))
    for h in range(q_heads):
        k = h // group
        cols = pl.ds(h * HEAD_DIM, HEAD_DIM)
        queries = qh[:, cols]
        numerator = jnp.zeros((rows, HEAD_DIM), f32)
        totals = jnp.zeros((rows, 1), f32)
        for j in range(seqs):
            keys = kv[j, :, k * HEAD_DIM:(k + 1) * HEAD_DIM]
            vals = kv[j, :, kv_width + k * HEAD_DIM:kv_width + (k + 1) * HEAD_DIM]
            scores = lax.dot_general(queries, keys, dims, preferred_element_type=f32)
            capped = softcap_limit * jnp.tanh(scores * (1.0 / softcap_limit))
            allowed = key_places[:, j * rows:(j + 1) * rows] <= places[:, :1]
            weight = jnp.where(allowed, jnp.exp(capped), 0.0)
            totals = totals + jnp.sum(weight, axis=1, keepdims=True)
            numerator = numerator + jnp.dot(weight.astype(bf16), vals, preferred_element_type=f32)
        att[:, cols] = (numerator / totals).astype(bf16)

    loads[3].wait()

    def chain_right(c, b, src):
        return remote(src, from_left.at[c, b], r_send.at[c, b], l_recv.at[c, b], right)

    def chain_left(c, b, src):
        return remote(src, from_right.at[c, b], l_send.at[c, b], r_recv.at[c, b], left)

    def project(c, carry):
        cols = pl.ds(c * width if isinstance(c, int) else pl.multiple_of(c * width, width), width)
        part[c] = jnp.dot(att[...], wo[:, cols], preferred_element_type=f32).astype(bf16)
        for k in range(tensors):
            far = tensors - 1 - k

            @pl.when(jnp.logical_and(z == 0, far > 0))
            def _():
                chain_right(c, far, part.at[c, block(far)]).start()

            @pl.when(jnp.logical_and(z == tensors - 1, k < tensors - 1))
            def _():
                chain_left(c, k, part.at[c, block(k)]).start()

            @pl.when(jnp.logical_and(z > 0, far > z))
            def _():
                chain_right(c, far, from_left.at[c, far]).wait_recv()
                from_left[c, far] = (from_left[c, far].astype(f32) + part[c, block(far)].astype(f32)).astype(bf16)
                chain_right(c, far, from_left.at[c, far]).start()

            @pl.when(jnp.logical_and(z < tensors - 1, k < z))
            def _():
                chain_left(c, k, from_right.at[c, k]).wait_recv()
                from_right[c, k] = (from_right[c, k].astype(f32) + part[c, block(k)].astype(f32)).astype(bf16)
                chain_left(c, k, from_right.at[c, k]).start()
        return carry

    if width % 128 == 0:
        lax.fori_loop(0, chunks, project, 0)
    else:
        for c in range(chunks):
            project(c, 0)

    own = block(z)

    def gather_sum(c, squares):
        total[c] = part[c, own].astype(f32)

        @pl.when(z > 0)
        def _():
            chain_right(c, z, from_left.at[c, z]).wait_recv()
            total[c] += from_left[c, z].astype(f32)

        @pl.when(z < tensors - 1)
        def _():
            chain_left(c, z, from_right.at[c, z]).wait_recv()
            total[c] += from_right[c, z].astype(f32)

        value = total[c]
        return squares + jnp.sum(value * value, axis=1, keepdims=True)

    squares = lax.fori_loop(0, chunks, gather_sum, jnp.zeros((part_rows, 1), f32))
    scaling = lax.rsqrt(squares / model + epsilon)

    def onward(c):
        return remote(fresh.at[c], x.at[c, own], next_send.at[c], x_recv.at[c, z], after)

    def share(c):
        return remote(fresh.at[c], landed.at[own], out_send.at[c], out_recv.at[z], {"tensor": c})

    for c in range(chunks):
        fresh[c] = (x[c, own].astype(f32) + total[c] * scaling * gain_out[c].astype(f32)).astype(bf16)

        @pl.when(s < sections - 1)
        def _():
            onward(c).start()

    for c in range(chunks):
        @pl.when(z != c)
        def _():
            share(c).start()

    landed[own] = fresh[z]
    for o in range(tensors):
        @pl.when(z != o)
        def _():
            remote(fresh.at[o], landed.at[block(o)], out_send.at[o], out_recv.at[o], {"tensor": o}).wait_recv()
    out[0, 0] = landed[...]

    for c in range(chunks):
        @pl.when(s < sections - 1)
        def _():
            onward(c).wait_send()

        @pl.when(z != c)
        def _():
            share(c).wait_send()

    for step in range(1, seqs):
        kv_copy(q, lax.rem(q + step, seqs)).wait_send()

    for o in range(tensors):
        @pl.when(jnp.logical_and(s == 0, jnp.logical_and(z < tensors - 1, o <= z)))
        def _():
            first_right(o, x.at[o]).wait_send()

        @pl.when(jnp.logical_and(s == 0, jnp.logical_and(z > 0, o >= z)))
        def _():
            first_left(o, x.at[o]).wait_send()

    def drain(c, carry):
        for o in range(tensors):
            @pl.when(jnp.logical_and(s > 0, jnp.logical_and(z < tensors - 1, o <= z)))
            def _():
                piece(c, o, x_right, right).wait_send()

            @pl.when(jnp.logical_and(s > 0, jnp.logical_and(z > 0, o >= z)))
            def _():
                piece(c, o, x_left, left).wait_send()

            @pl.when(o > z)
            def _():
                chain_right(c, o, from_left.at[c, o]).wait_send()

            @pl.when(o < z)
            def _():
                chain_left(c, o, from_right.at[c, o]).wait_send()
        return carry

    lax.fori_loop(0, chunks, drain, 0)


def body(sections, seqs, tensors, states_in, span_order, pre_gain, w_query, w_key, w_value, w_out, post_gain):
    _, rows, width = states_in.shape
    model = pre_gain.shape[1]
    chunks = model // width
    part_rows = rows // tensors
    q_width, kv_width = w_query.shape[2], w_key.shape[2]
    vmem = pl.BlockSpec(memory_space=pltpu.VMEM)
    hbm = pl.BlockSpec(memory_space=pl.ANY)
    smem = pl.BlockSpec(memory_space=pltpu.SMEM)
    dma = pltpu.SemaphoreType.DMA
    grid2 = (chunks, tensors)
    return pl.pallas_call(
        functools.partial(kernel, sections, seqs, tensors),
        out_shape=jax.ShapeDtypeStruct((1, 1, rows, width), bf16),
        in_specs=[vmem, smem, vmem, hbm, hbm, hbm, hbm, vmem],
        out_specs=vmem,
        scratch_shapes=[
            pltpu.VMEM((model, q_width), bf16),
            pltpu.VMEM((model, kv_width), bf16),
            pltpu.VMEM((model, kv_width), bf16),
            pltpu.VMEM((q_width, model), bf16),
            pltpu.VMEM((chunks, rows, width), bf16),
            pltpu.VMEM((rows, q_width), f32),
            pltpu.VMEM((rows, 2 * kv_width), f32),
            pltpu.VMEM((seqs, rows, 2 * kv_width), bf16),
            pltpu.VMEM((rows, q_width), bf16),
            pltpu.VMEM((rows, q_width), bf16),
            pltpu.VMEM((chunks, rows, width), bf16),
            pltpu.VMEM((chunks, tensors, part_rows, width), bf16),
            pltpu.VMEM((chunks, tensors, part_rows, width), bf16),
            pltpu.VMEM((chunks, part_rows, width), f32),
            pltpu.VMEM((chunks, part_rows, width), bf16),
            pltpu.VMEM((rows, width), bf16),
            dma((4,)),
            dma((tensors,)), dma((tensors,)), dma((tensors,)),
            dma(grid2), dma(grid2), dma(grid2),
            dma((seqs,)), dma((seqs,)),
            dma(grid2), dma(grid2), dma(grid2), dma(grid2),
            dma((chunks,)), dma((tensors,)), dma((tensors,)),
        ],
        compiler_params=pltpu.CompilerParams(
            collective_id=0, has_side_effects=True, vmem_limit_bytes=60 * 1024 * 1024
        ),
    )(
        states_in, span_order, pre_gain.reshape(chunks, 1, width), w_query, w_key, w_value, w_out,
        post_gain.reshape(chunks, 1, width),
    )


def solution(mesh):
    in_specs = (
        P(None, "seq", "tensor"),
        P(),
        P("section", None),
        P("section", None, "tensor"),
        P("section", None, "tensor"),
        P("section", None, "tensor"),
        P("section", "tensor", None),
        P("section", None),
    )
    out_specs = P("section", None, "seq", "tensor")
    sizes = (mesh.shape["section"], mesh.shape["seq"], mesh.shape["tensor"])
    return jax.shard_map(
        functools.partial(body, *sizes), mesh=mesh, in_specs=in_specs, out_specs=out_specs, check_vma=False
    )
```

time: 500 us -> 347 us (0.69)
  Pallas kernels: 0 us -> 345 us
  waiting for transfers between devices: 337 us -> 0 us
  matrix products: 68.5 us -> 0 us
  other arithmetic: 26.3 us -> 0 us
  local copies, waits for them, and re-layouts: 25 us -> 1.7 us
  blocking collectives: 16.1 us -> 0 us
  between operations: 13.4 us -> 0.01 us
  starting transfers between devices: 5.48 us -> 0 us
    pallas_call x0 -> x1, Pallas kernels: none -> 345 us  [body(): pl.pallas_call(functools.partial(kernel, sections, seqs, tensors), out_sh...]
    psum x4 -> x0, waiting for transfers between devices: 217 us -> none  [layer(): lax.psum(partial_value.astype(jnp.bfloat16), 'tensor').astype(jnp.float32)]
    ppermute x4 -> x0, waiting for transfers between devices: 112 us -> none  [from_behind(): lax.ppermute(value, axis, [(source, source + steps) for source in range(f...]
    dot_general x24 -> x0, matrix products: 68.5 us -> none  [the longest x4 24.7 us: layer(): jnp.dot(attended, w_out[0], preferred_element_type=jnp.float32)]
    unnamed x6 -> x1, local copies, waits for them, and re-layouts: 20.2 us -> 1.7 us
    all_gather x8 -> x0, blocking collectives: 16.1 us -> none  [the longest x4 8.09 us: layer(): key_piece = lax.all_gather(key_rows, 'seq', axis=0, tiled=True)]
    reduce_sum x13 -> x0, other arithmetic: 15.1 us -> none  [the longest x4 7.68 us: layer(): jnp.mean(stream * stream, axis=1, keepdims=True) + epsilon]
    convert_element_type x6 -> x0, other arithmetic: 8.51 us -> none  [the longest x4 7.06 us: layer(): new_full = (stream + projected * scaling * gain_out).astype(jnp.bfloat16)]
  transfers between devices with their start and end apart: 12 -> 0, of which waited for: 12 -> 0; matrix products, arithmetic and copies ran while one was open for 1% -> 0% of each run, Pallas kernels for 0% -> 0%
where the time goes in v1:
time: 347 us
  Pallas kernels  345 us (99%)
    pallas_call x1, Pallas kernels, body(): pl.pallas_call(functools.partial(kernel, sections, seqs, tensors), out_sh...  345 us

profile of v1, /device:TPU:30, one launch (start us, length us, event | category | flops | bytes accessed | tf_op | source)
XLA Modules:
  0.0 346.5 jit_solution(17839067328757668120)
XLA Ops:
  0.0 344.8 %shard_map.82 = bf16[1,1,128,1152]{3,2,1,0:T(8,128)(2,1)} custom-call(bf16[1,128,1152]{2,1,0:T(8,128)(2,1)} %states.1, s32[4]{0:T(128)} %order.1, bf16[4,1,1152]{2,1,0:T(2,128)(2,1)} %bitcast.2, bf16[1,4608,1024]{2,1,0:T(8,128)(2,1)} %wq_hbm.1, bf16[1,4608,512]{2,1,0:T(8,128)(2,1)} %wk_hbm.1, bf16[1,4608,512]{2,1,0:T(8,128)(2,1)} %wv_hbm.1, ...), custom_call_target="tpu_custom_call" | custom-call | tf_op jit(solution)/shard_map/pallas_call | solution.py:360
  344.8 1.7 copy.10

commit v2 on v1

v2 whole, which is shorter than its diff:
```python
import functools
import math

import jax
import jax.numpy as jnp
from jax import lax
from jax.experimental import pallas as pl
from jax.experimental.pallas import tpu as pltpu
from jax.sharding import PartitionSpec as P

HEAD_DIM = 128

softcap_limit = 50.0
query_scale = 144.0 ** (-0.5)
epsilon = 1e-06
rotary_base = 10000.0

MESH = pl.DeviceIdType.MESH
f32 = jnp.float32
bf16 = jnp.bfloat16


def kernel(
    sections, seqs, tensors,
    states, order, gain_in, wq_hbm, wk_hbm, wv_hbm, wo_hbm, gain_out, out,
    wq, wk, wv, wo, x, acc_q, acc_kv, kv, qh, att, part, from_left, from_right, total, fresh, landed,
    relay, raw, back, cos_ref, sin_ref,
    w_sem, x_recv, x_right, x_left, relay_recv, deliver_send, kv_send, kv_recv,
    l_recv, r_recv, l_send, r_send, raw_send, raw_recv, back_send, back_recv, next_send, out_send, out_recv,
):
    t = lax.axis_index("section")
    q = lax.axis_index("seq")
    z = lax.axis_index("tensor")
    _, rows, width = states.shape
    chunks = x.shape[0]
    model = chunks * width
    part_rows = rows // tensors
    q_width = wq.shape[1]
    kv_width = wk.shape[1]
    q_heads = q_width // HEAD_DIM
    kv_heads = kv_width // HEAD_DIM
    group = q_heads // kv_heads
    span_count = order.shape[0]
    span = rows * seqs // span_count
    roles = 2

    def helper(s, r):
        return s + 1 - 2 * lax.rem(s, 2) if r == 0 else lax.rem(s + sections // 2, sections)

    def remote(src, dst, send, recv, device):
        return pltpu.make_async_remote_copy(
            src_ref=src, dst_ref=dst, send_sem=send, recv_sem=recv, device_id=device, device_id_type=MESH
        )

    right = {"tensor": lax.rem(z + 1, tensors)}
    left = {"tensor": lax.rem(z + tensors - 1, tensors)}

    loads = [
        pltpu.make_async_copy(src.at[0], dst, w_sem.at[i])
        for i, (src, dst) in enumerate(((wk_hbm, wk), (wv_hbm, wv), (wq_hbm, wq), (wo_hbm, wo)))
    ]
    for load in loads:
        load.start()

    barrier = pltpu.get_barrier_semaphore()
    for axis, here, count in (("tensor", z, tensors), ("seq", q, seqs), ("section", t, sections)):
        for step in range(1, count):
            pl.semaphore_signal(barrier, inc=1, device_id={axis: lax.rem(here + step, count)}, device_id_type=MESH)
    pl.semaphore_wait(barrier, tensors + seqs + sections - 3)

    def block(o):
        return pl.ds(pl.multiple_of(o * part_rows, part_rows), part_rows)

    def piece(s, c, o):
        first = 1 - lax.div(s + sections - 1, sections)
        return x.at[c + first * (o - c), block(o + first * (c - o))]

    def gather(cs, ref, recv, ready, arrived):
        for d in range(tensors):
            for c in cs:
                def step(o, go_right, go_left):
                    if go_right:
                        @pl.when(z < tensors - 1)
                        def _():
                            remote(ref(c, o), ref(c, o), x_right.at[c, o], recv.at[c, o], right).start()
                    if go_left:
                        @pl.when(z > 0)
                        def _():
                            remote(ref(c, o), ref(c, o), x_left.at[c, o], recv.at[c, o], left).start()

                if d == 0:
                    ready(c)
                    step(z, True, True)
                    arrived(z)
                else:
                    @pl.when(z >= d)
                    def _():
                        remote(ref(c, z - d), ref(c, z - d), x_right.at[c, z - d], recv.at[c, z - d], right).wait_recv()
                        step(z - d, True, False)
                        arrived(z - d)

                    @pl.when(z + d < tensors)
                    def _():
                        remote(ref(c, z + d), ref(c, z + d), x_left.at[c, z + d], recv.at[c, z + d], left).wait_recv()
                        step(z + d, False, True)
                        arrived(z + d)

    def chain_right(c, b, src):
        return remote(src, from_left.at[c, b], r_send.at[c, b], l_recv.at[c, b], right)

    def chain_left(c, b, src):
        return remote(src, from_right.at[c, b], l_send.at[c, b], r_recv.at[c, b], left)

    def chain(cs, mine):
        for k in range(tensors):
            far = tensors - 1 - k
            for c in cs:
                @pl.when(jnp.logical_and(z == 0, far > 0))
                def _():
                    chain_right(c, far, mine(c, far)).start()

                @pl.when(jnp.logical_and(z == tensors - 1, k < tensors - 1))
                def _():
                    chain_left(c, k, mine(c, k)).start()

                @pl.when(jnp.logical_and(z > 0, far > z))
                def _():
                    chain_right(c, far, from_left.at[c, far]).wait_recv()
                    from_left[c, far] = (from_left[c, far].astype(f32) + mine(c, far)[...].astype(f32)).astype(bf16)
                    chain_right(c, far, from_left.at[c, far]).start()

                @pl.when(jnp.logical_and(z < tensors - 1, k < z))
                def _():
                    chain_left(c, k, from_right.at[c, k]).wait_recv()
                    from_right[c, k] = (from_right[c, k].astype(f32) + mine(c, k)[...].astype(f32)).astype(bf16)
                    chain_left(c, k, from_right.at[c, k]).start()

    def chain_end(c, mine):
        total[c] = mine(c, z)[...].astype(f32)

        @pl.when(z > 0)
        def _():
            chain_right(c, z, from_left.at[c, z]).wait_recv()
            total[c] += from_left[c, z].astype(f32)

        @pl.when(z < tensors - 1)
        def _():
            chain_left(c, z, from_right.at[c, z]).wait_recv()
            total[c] += from_right[c, z].astype(f32)

    def relay_ref(c, o):
        return relay.at[c, o]

    def deliver(s, r, o):
        return remote(relay.at[r, o], piece(s, r, o), deliver_send.at[r, o], x_recv.at[r, o], {"section": s})

    def onward_relay(r):
        goal = lax.rem(t + 1, sections)
        return remote(fresh.at[r], relay.at[r, z], next_send.at[r], relay_recv.at[r, z], {"section": helper(goal, r)})

    def onward(c):
        goal = lax.rem(t + 1, sections)
        return remote(fresh.at[c], x.at[c, block(z)], next_send.at[c], x_recv.at[c, z], {"section": goal})

    def raw_copy(r):
        return remote(part.at[r], raw.at[r], raw_send.at[r], raw_recv.at[r], {"section": helper(t, r)})

    def back_copy(r):
        return remote(relay.at[roles + r, 0], back.at[r], back_send.at[r], back_recv.at[r], {"section": helper(t, r)})

    def raw_block(c, b):
        return raw.at[c, block(b)]

    def help_gather(s, r):
        def ready(c):
            @pl.when(s == 0)
            def _():
                relay[r, z] = states[0, r * part_rows:(r + 1) * part_rows, :]

            @pl.when(jnp.logical_and(s > 0, s == t + 1))
            def _():
                relay[r, z] = fresh[r]

            @pl.when(jnp.logical_and(s > 0, s != t + 1))
            def _():
                onward_relay(r).wait_recv()

        gather([r], relay_ref, relay_recv, ready, lambda o: deliver(s, r, o).start())

    def help_reduce(r):
        raw_copy(r).wait_recv()
        chain([r], raw_block)
        chain_end(r, raw_block)
        relay[roles + r, 0] = total[r].astype(bf16)
        back_copy(r).start()

    half = HEAD_DIM // 2

    def positions():
        row = lax.broadcasted_iota(jnp.int32, (rows, HEAD_DIM), 0) + q * rows
        starts = jnp.zeros((rows, HEAD_DIM), jnp.int32)
        key_col = lax.broadcasted_iota(jnp.int32, (1, rows * seqs), 1)
        key_starts = jnp.zeros((1, rows * seqs), jnp.int32)
        for j in range(span_count):
            begin = order[j] * span
            starts = jnp.where(row // span == j, begin, starts)
            key_starts = jnp.where(key_col // span == j, begin, key_starts)
        return starts + row % span, key_starts + key_col % span

    def rope(u):
        return u * cos_ref[...] + pltpu.roll(u, half, 1) * sin_ref[...]

    def tables():
        places, _ = positions()
        lane = lax.broadcasted_iota(jnp.int32, (rows, HEAD_DIM), 1)
        inverse = jnp.exp((lane % half).astype(f32) * (-2.0 / HEAD_DIM * math.log(rotary_base)))
        angles = places.astype(f32) * inverse
        cos_ref[...] = jnp.cos(angles)
        sin_ref[...] = jnp.sin(angles) * jnp.where(lane < half, -1.0, 1.0)

    def kv_copy(j, device):
        return remote(kv.at[j], kv.at[j], kv_send.at[device], kv_recv.at[j], {"seq": device})

    def share(c):
        return remote(fresh.at[c], landed.at[block(z)], out_send.at[c], out_recv.at[z], {"tensor": c})

    def part_block(c, b):
        return part.at[c, block(b)]

    def layer():
        line = list(range(roles, chunks))

        def own_piece(c, o):
            return piece(t, c, o)

        def ready(c):
            @pl.when(t > 0)
            def _():
                onward(c).wait_recv()

        gather(line, own_piece, x_recv, ready, lambda o: None)
        for r in range(roles):
            for o in range(tensors):
                deliver(t, r, o).wait_recv()

        acc_q[...] = jnp.zeros_like(acc_q)
        acc_kv[...] = jnp.zeros_like(acc_kv)
        for load in loads[:3]:
            load.wait()

        def take_chunk(c, squares):
            stream = x[c].astype(f32)
            squares = squares + jnp.sum(stream * stream, axis=1, keepdims=True)
            scaled = (stream * gain_in[c].astype(f32)).astype(bf16)
            depth = pl.ds(pl.multiple_of(c * width, width), width)
            acc_kv[:, :kv_width] += jnp.dot(scaled, wk[depth, :], preferred_element_type=f32)
            acc_kv[:, kv_width:] += jnp.dot(scaled, wv[depth, :], preferred_element_type=f32)
            acc_q[...] += jnp.dot(scaled, wq[depth, :], preferred_element_type=f32)
            return squares

        squares = lax.fori_loop(0, chunks, take_chunk, jnp.zeros((rows, 1), f32))
        scale = lax.rsqrt(squares / model + epsilon)
        for k in range(kv_heads):
            cols = pl.ds(k * HEAD_DIM, HEAD_DIM)
            kv[q, :, cols] = rope(acc_kv[:, cols] * scale).astype(bf16)
        kv[q, :, kv_width:] = (acc_kv[:, kv_width:] * scale).astype(bf16)
        for step in range(1, seqs):
            kv_copy(q, lax.rem(q + step, seqs)).start()
        for h in range(q_heads):
            cols = pl.ds(h * HEAD_DIM, HEAD_DIM)
            qh[:, cols] = (rope(acc_q[:, cols] * scale) * query_scale).astype(bf16)
        for step in range(1, seqs):
            other = lax.rem(q + step, seqs)
            kv_copy(other, other).wait_recv()

        places, key_places = positions()
        dims = (((1,), (1,)), ((), ()))
        for h in range(q_heads):
            k = h // group
            cols = pl.ds(h * HEAD_DIM, HEAD_DIM)
            queries = qh[:, cols]
            numerator = jnp.zeros((rows, HEAD_DIM), f32)
            totals = jnp.zeros((rows, 1), f32)
            for j in range(seqs):
                keys = kv[j, :, k * HEAD_DIM:(k + 1) * HEAD_DIM]
                vals = kv[j, :, kv_width + k * HEAD_DIM:kv_width + (k + 1) * HEAD_DIM]
                scores = lax.dot_general(queries, keys, dims, preferred_element_type=f32)
                capped = softcap_limit * jnp.tanh(scores * (1.0 / softcap_limit))
                allowed = key_places[:, j * rows:(j + 1) * rows] <= places[:, :1]
                weight = jnp.where(allowed, jnp.exp(capped), 0.0)
                totals = totals + jnp.sum(weight, axis=1, keepdims=True)
                numerator = numerator + jnp.dot(weight.astype(bf16), vals, preferred_element_type=f32)
            att[:, cols] = (numerator / totals).astype(bf16)

        loads[3].wait()
        for c in range(chunks):
            part[c] = jnp.dot(
                att[...], wo[:, c * width:(c + 1) * width], preferred_element_type=f32
            ).astype(bf16)
            if c < roles:
                raw_copy(c).start()
        chain(line, part_block)
        for c in line:
            chain_end(c, part_block)
        squares = jnp.zeros((part_rows, 1), f32)
        for r in range(roles):
            back_copy(r).wait_recv()
            total[r] = back[r].astype(f32)
        for c in range(chunks):
            squares = squares + jnp.sum(total[c] * total[c], axis=1, keepdims=True)
        scaling = lax.rsqrt(squares / model + epsilon)
        for c in range(chunks):
            fresh[c] = (x[c, block(z)].astype(f32) + total[c] * scaling * gain_out[c].astype(f32)).astype(bf16)
            if c < roles:
                @pl.when(jnp.logical_and(t < sections - 1, helper(lax.rem(t + 1, sections), c) != t))
                def _():
                    onward_relay(c).start()
            else:
                @pl.when(t < sections - 1)
                def _():
                    onward(c).start()
        for c in range(chunks):
            @pl.when(z != c)
            def _():
                share(c).start()

    @pl.when(t == 0)
    def _():
        x[z, roles * part_rows:, :] = states[0, roles * part_rows:, :]

    tables()

    def turn(s, carry):
        @pl.when(s == t)
        def _():
            layer()

        for r in range(roles):
            @pl.when(s == helper(t, r))
            def _():
                help_gather(s, r)
                help_reduce(r)
        return carry

    lax.fori_loop(0, sections, turn, 0)

    own = block(z)
    landed[own] = fresh[z]
    for o in range(tensors):
        @pl.when(z != o)
        def _():
            remote(fresh.at[o], landed.at[block(o)], out_send.at[o], out_recv.at[o], {"tensor": o}).wait_recv()
    out[0, 0] = landed[...]

    for c in range(chunks):
        if c < roles:
            @pl.when(jnp.logical_and(t < sections - 1, helper(lax.rem(t + 1, sections), c) != t))
            def _():
                onward_relay(c).wait_send()
            raw_copy(c).wait_send()
            back_copy(c).wait_send()
            for o in range(tensors):
                deliver(helper(t, c), c, o).wait_send()
        else:
            @pl.when(t < sections - 1)
            def _():
                onward(c).wait_send()

        @pl.when(z != c)
        def _():
            share(c).wait_send()

    for step in range(1, seqs):
        kv_copy(q, lax.rem(q + step, seqs)).wait_send()

    def drain(c, carry):
        for o in range(tensors):
            @pl.when(jnp.logical_and(z < tensors - 1, o <= z))
            def _():
                remote(relay.at[0, o], relay.at[0, o], x_right.at[c, o], x_recv.at[c, o], right).wait_send()

            @pl.when(jnp.logical_and(z > 0, o >= z))
            def _():
                remote(relay.at[0, o], relay.at[0, o], x_left.at[c, o], x_recv.at[c, o], left).wait_send()

            @pl.when(o > z)
            def _():
                chain_right(c, o, from_left.at[c, o]).wait_send()

            @pl.when(o < z)
            def _():
                chain_left(c, o, from_right.at[c, o]).wait_send()
        return carry

    lax.fori_loop(0, chunks, drain, 0)


def body(sections, seqs, tensors, states_in, span_order, pre_gain, w_query, w_key, w_value, w_out, post_gain):
    _, rows, width = states_in.shape
    model = pre_gain.shape[1]
    chunks = model // width
    part_rows = rows // tensors
    q_width, kv_width = w_query.shape[2], w_key.shape[2]
    vmem = pl.BlockSpec(memory_space=pltpu.VMEM)
    hbm = pl.BlockSpec(memory_space=pl.ANY)
    smem = pl.BlockSpec(memory_space=pltpu.SMEM)
    dma = pltpu.SemaphoreType.DMA
    grid2 = (chunks, tensors)
    return pl.pallas_call(
        functools.partial(kernel, sections, seqs, tensors),
        out_shape=jax.ShapeDtypeStruct((1, 1, rows, width), bf16),
        in_specs=[vmem, smem, vmem, hbm, hbm, hbm, hbm, vmem],
        out_specs=vmem,
        scratch_shapes=[
            pltpu.VMEM((model, q_width), bf16),
            pltpu.VMEM((model, kv_width), bf16),
            pltpu.VMEM((model, kv_width), bf16),
            pltpu.VMEM((q_width, model), bf16),
            pltpu.VMEM((chunks, rows, width), bf16),
            pltpu.VMEM((rows, q_width), f32),
            pltpu.VMEM((rows, 2 * kv_width), f32),
            pltpu.VMEM((seqs, rows, 2 * kv_width), bf16),
            pltpu.VMEM((rows, q_width), bf16),
            pltpu.VMEM((rows, q_width), bf16),
            pltpu.VMEM((chunks, rows, width), bf16),
            pltpu.VMEM((chunks, tensors, part_rows, width), bf16),
            pltpu.VMEM((chunks, tensors, part_rows, width), bf16),
            pltpu.VMEM((chunks, part_rows, width), f32),
            pltpu.VMEM((chunks, part_rows, width), bf16),
            pltpu.VMEM((rows, width), bf16),
            pltpu.VMEM((4, tensors, part_rows, width), bf16),
            pltpu.VMEM((2, rows, width), bf16),
            pltpu.VMEM((2, part_rows, width), bf16),
            pltpu.VMEM((rows, HEAD_DIM), f32),
            pltpu.VMEM((rows, HEAD_DIM), f32),
            dma((4,)),
            dma(grid2), dma(grid2), dma(grid2),
            dma((2, tensors)), dma((2, tensors)),
            dma((seqs,)), dma((seqs,)),
            dma(grid2), dma(grid2), dma(grid2), dma(grid2),
            dma((2,)), dma((2,)), dma((2,)), dma((2,)),
            dma((chunks,)), dma((tensors,)), dma((tensors,)),
        ],
        compiler_params=pltpu.CompilerParams(
            collective_id=0, has_side_effects=True, vmem_limit_bytes=60 * 1024 * 1024
        ),
    )(
        states_in, span_order, pre_gain.reshape(chunks, 1, width), w_query, w_key, w_value, w_out,
        post_gain.reshape(chunks, 1, width),
    )


def solution(mesh):
    in_specs = (
        P(None, "seq", "tensor"),
        P(),
        P("section", None),
        P("section", None, "tensor"),
        P("section", None, "tensor"),
        P("section", None, "tensor"),
        P("section", "tensor", None),
        P("section", None),
    )
    out_specs = P("section", None, "seq", "tensor")
    sizes = (mesh.shape["section"], mesh.shape["seq"], mesh.shape["tensor"])
    return jax.shard_map(
        functools.partial(body, *sizes), mesh=mesh, in_specs=in_specs, out_specs=out_specs, check_vma=False
    )
```

time: 347 us -> 204 us (0.59)
  Pallas kernels: 345 us -> 202 us
    pallas_call x1, Pallas kernels: 345 us -> 202 us  [body(): pl.pallas_call(functools.partial(kernel, sections, seqs, tensors), out_sh...]
where the time goes in v2:
time: 204 us
  Pallas kernels  202 us (99%)
    pallas_call x1, Pallas kernels, body(): pl.pallas_call(functools.partial(kernel, sections, seqs, tensors), out_sh...  202 us

profile of v2, /device:TPU:30, one launch (start us, length us, event | category | flops | bytes accessed | tf_op | source)
XLA Modules:
  0.0 203.9 jit_solution(18147246091895571658)
XLA Ops:
  0.0 202.2 %shard_map.82 = bf16[1,1,128,1152]{3,2,1,0:T(8,128)(2,1)} custom-call(bf16[1,128,1152]{2,1,0:T(8,128)(2,1)} %states.1, s32[4]{0:T(128)} %order.1, bf16[4,1,1152]{2,1,0:T(2,128)(2,1)} %bitcast.2, bf16[1,4608,1024]{2,1,0:T(8,128)(2,1)} %wq_hbm.1, bf16[1,4608,512]{2,1,0:T(8,128)(2,1)} %wk_hbm.1, bf16[1,4608,512]{2,1,0:T(8,128)(2,1)} %wv_hbm.1, ...), custom_call_target="tpu_custom_call" | custom-call | tf_op jit(solution)/shard_map/pallas_call | solution.py:409
  202.2 1.7 copy.10

commit v3 on v2

--- a/solution.py
+++ b/solution.py
@@ -112,28 +112,42 @@
         return remote(src, from_right.at[c, b], l_send.at[c, b], r_recv.at[c, b], left)
 
     def chain(cs, mine):
+        def rightward(c, far):
+            @pl.when(jnp.logical_and(z == 0, far > 0))
+            def _():
+                chain_right(c, far, mine(c, far)).start()
+
+            @pl.when(jnp.logical_and(z > 0, far > z))
+            def _():
+                chain_right(c, far, from_left.at[c, far]).wait_recv()
+                from_left[c, far] = (from_left[c, far].astype(f32) + mine(c, far)[...].astype(f32)).astype(bf16)
+                chain_right(c, far, from_left.at[c, far]).start()
+
+        def leftward(c, k):
+            @pl.when(jnp.logical_and(z == tensors - 1, k < tensors - 1))
+            def _():
+                chain_left(c, k, mine(c, k)).start()
+
+            @pl.when(jnp.logical_and(z < tensors - 1, k < z))
+            def _():
+                chain_left(c, k, from_right.at[c, k]).wait_recv()
+                from_right[c, k] = (from_right[c, k].astype(f32) + mine(c, k)[...].astype(f32)).astype(bf16)
+                chain_left(c, k, from_right.at[c, k]).start()
+
         for k in range(tensors):
-            far = tensors - 1 - k
-            for c in cs:
-                @pl.when(jnp.logical_and(z == 0, far > 0))
-                def _():
-                    chain_right(c, far, mine(c, far)).start()
-
-                @pl.when(jnp.logical_and(z == tensors - 1, k < tensors - 1))
-                def _():
-                    chain_left(c, k, mine(c, k)).start()
-
-                @pl.when(jnp.logical_and(z > 0, far > z))
-                def _():
-                    chain_right(c, far, from_left.at[c, far]).wait_recv()
-                    from_left[c, far] = (from_left[c, far].astype(f32) + mine(c, far)[...].astype(f32)).astype(bf16)
-                    chain_right(c, far, from_left.at[c, far]).start()
-
-                @pl.when(jnp.logical_and(z < tensors - 1, k < z))
-                def _():
-                    chain_left(c, k, from_right.at[c, k]).wait_recv()
-                    from_right[c, k] = (from_right[c, k].astype(f32) + mine(c, k)[...].astype(f32)).astype(bf16)
-                    chain_left(c, k, from_right.at[c, k]).start()
+            @pl.when(z < tensors // 2)
+            def _():
+                for c in cs:
+                    rightward(c, tensors - 1 - k)
+                for c in cs:
+                    leftward(c, k)
+
+            @pl.when(z >= tensors // 2)
+            def _():
+                for c in cs:
+                    leftward(c, k)
+                for c in cs:
+                    rightward(c, tensors - 1 - k)
 
     def chain_end(c, mine):
         total[c] = mine(c, z)[...].astype(f32)
@@ -162,13 +176,16 @@
         goal = lax.rem(t + 1, sections)
         return remote(fresh.at[c], x.at[c, block(z)], next_send.at[c], x_recv.at[c, z], {"section": goal})
 
-    def raw_copy(r):
-        return remote(part.at[r], raw.at[r], raw_send.at[r], raw_recv.at[r], {"section": helper(t, r)})
+    def raw_copy(r, b):
+        return remote(
+            part.at[r, block(b)], raw.at[r, block(b)], raw_send.at[r, b], raw_recv.at[r, b], {"section": helper(t, r)}
+        )
 
     def back_copy(r):
         return remote(relay.at[roles + r, 0], back.at[r], back_send.at[r], back_recv.at[r], {"section": helper(t, r)})
 
     def raw_block(c, b):
+        raw_copy(c, b).wait_recv()
         return raw.at[c, block(b)]
 
     def help_gather(s, r):
@@ -188,7 +205,6 @@
         gather([r], relay_ref, relay_recv, ready, lambda o: deliver(s, r, o).start())
 
     def help_reduce(r):
-        raw_copy(r).wait_recv()
         chain([r], raw_block)
         chain_end(r, raw_block)
         relay[roles + r, 0] = total[r].astype(bf16)
@@ -239,9 +255,15 @@
                 onward(c).wait_recv()
 
         gather(line, own_piece, x_recv, ready, lambda o: None)
-        for r in range(roles):
+
+        def delivered(r):
             for o in range(tensors):
                 deliver(t, r, o).wait_recv()
+
+        @pl.when(t == 0)
+        def _():
+            for r in range(roles):
+                delivered(r)
 
         acc_q[...] = jnp.zeros_like(acc_q)
         acc_kv[...] = jnp.zeros_like(acc_kv)
@@ -258,7 +280,13 @@
             acc_q[...] += jnp.dot(scaled, wq[depth, :], preferred_element_type=f32)
             return squares
 
-        squares = lax.fori_loop(0, chunks, take_chunk, jnp.zeros((rows, 1), f32))
+        squares = lax.fori_loop(roles, chunks, take_chunk, jnp.zeros((rows, 1), f32))
+        for r in range(roles):
+            @pl.when(t > 0)
+            def _():
+                delivered(r)
+
+        squares = lax.fori_loop(0, roles, take_chunk, squares)
         scale = lax.rsqrt(squares / model + epsilon)
         for k in range(kv_heads):
             cols = pl.ds(k * HEAD_DIM, HEAD_DIM)
@@ -298,7 +326,8 @@
                 att[...], wo[:, c * width:(c + 1) * width], preferred_element_type=f32
             ).astype(bf16)
             if c < roles:
-                raw_copy(c).start()
+                for k in range(tensors):
+                    raw_copy(c, k // 2 if k % 2 else tensors - 1 - k // 2).start()
         chain(line, part_block)
         for c in line:
             chain_end(c, part_block)
@@ -357,10 +386,10 @@
             @pl.when(jnp.logical_and(t < sections - 1, helper(lax.rem(t + 1, sections), c) != t))
             def _():
                 onward_relay(c).wait_send()
-            raw_copy(c).wait_send()
             back_copy(c).wait_send()
             for o in range(tensors):
                 deliver(helper(t, c), c, o).wait_send()
+                raw_copy(c, o).wait_send()
         else:
             @pl.when(t < sections - 1)
             def _():
@@ -438,7 +467,7 @@
             dma((2, tensors)), dma((2, tensors)),
             dma((seqs,)), dma((seqs,)),
             dma(grid2), dma(grid2), dma(grid2), dma(grid2),
-            dma((2,)), dma((2,)), dma((2,)), dma((2,)),
+            dma((2, tensors)), dma((2, tensors)), dma((2,)), dma((2,)),
             dma((chunks,)), dma((tensors,)), dma((tensors,)),
         ],
         compiler_params=pltpu.CompilerParams(

time: 204 us -> 182 us (0.89)
  Pallas kernels: 202 us -> 180 us
    pallas_call x1, Pallas kernels: 202 us -> 180 us  [body(): pl.pallas_call(functools.partial(kernel, sections, seqs, tensors), out_sh...]
where the time goes in v3:
time: 182 us
  Pallas kernels  180 us (99%)
    pallas_call x1, Pallas kernels, body(): pl.pallas_call(functools.partial(kernel, sections, seqs, tensors), out_sh...  180 us

profile of v3, /device:TPU:30, one launch (start us, length us, event | category | flops | bytes accessed | tf_op | source)
XLA Modules:
  0.0 181.6 jit_solution(9657029992942333355)
XLA Ops:
  0.0 179.9 %shard_map.82 = bf16[1,1,128,1152]{3,2,1,0:T(8,128)(2,1)} custom-call(bf16[1,128,1152]{2,1,0:T(8,128)(2,1)} %states.1, s32[4]{0:T(128)} %order.1, bf16[4,1,1152]{2,1,0:T(2,128)(2,1)} %bitcast.2, bf16[1,4608,1024]{2,1,0:T(8,128)(2,1)} %wq_hbm.1, bf16[1,4608,512]{2,1,0:T(8,128)(2,1)} %wk_hbm.1, bf16[1,4608,512]{2,1,0:T(8,128)(2,1)} %wv_hbm.1, ...), custom_call_target="tpu_custom_call" | custom-call | tf_op jit(solution)/shard_map/pallas_call | solution.py:438
  179.9 1.7 copy.10
